TPU v7x, 32 devices: a whole 2x2x4 slice. The times are simulated.
32 devices in a mesh: gz: 8 (over z, y), ga: 4 (over x, core).
Axes of the slice: x: 2, y: 2, z: 4, core: 2. Of those that a mesh axis runs over, the one named last changes fastest.
Arguments:
- solution: float32 [64, 256, 256], P(('gz', 'ga')), may hold values from -6 to 6
- residual: float32 [64, 256, 256], P(('gz', 'ga')), may hold values from -40 to 40
- direction: float32 [64, 256, 256], P(('gz', 'ga')), may hold values from -40 to 40
Outputs:
- solution_out: float32 [64, 256, 256], P(('gz', 'ga'))
- residual_out: float32 [64, 256, 256], P(('gz', 'ga'))
- direction_out: float32 [64, 256, 256], P(('gz', 'ga'))
All inputs are finite; a program needn't handle non-finite values.
Results may differ from a plain program's by a relative error of at most 0.0003.
Values sent between devices are 32-bit elements; how exact they have to be, the bound alone decides.
A program may use at most 128 MiB of HBM per device.

v0:
```python
import functools

import jax
import jax.numpy as jnp
import numpy as np
from jax import lax
from jax.experimental import pallas as pl
from jax.experimental.pallas import tpu as pltpu
from jax.sharding import PartitionSpec as P

S = 8
MESH = pl.DeviceIdType.MESH
first_scale = -1.0 / 6.0
next_scale = -1.0 / 3.0
SIDE = 24
LANES = 128


def change_matrix(steps):
    count = 2 * steps + 1
    table = np.zeros((count, count), np.float64)
    for offset, length in ((0, steps + 1), (steps + 1, steps)):
        for power in range(length - 1):
            column = offset + power
            table[column, column] = 6.0
            if power == 0:
                table[column + 1, column] = 6.0
            else:
                table[column + 1, column] = 3.0
                table[column - 1, column] = 3.0
    return table


def dd(power, odd):
    return 2 * power + odd


def rr(power, odd):
    return 2 * S + 1 + 2 * power + odd


def dr(power, odd):
    return 4 * S + 2 * power + odd


COUNT = 6 * S


def gram_tables():
    def moment(kind, order):
        half, odd = order // 2, order % 2
        row = np.zeros(COUNT)
        row[kind(half, odd)] += 2.0
        row[kind(0, odd)] -= 1.0
        return row

    size = 2 * S + 1
    table = np.zeros((COUNT, size, size))
    for i in range(size):
        for j in range(size):
            a, b = (i if i <= S else i - S - 1), (j if j <= S else j - S - 1)
            kind = dd if (i <= S and j <= S) else rr if (i > S and j > S) else dr
            table[:, i, j] = 0.5 * (moment(kind, a + b) + moment(kind, abs(a - b)))
    moved = table @ change_matrix(S)

    def padded(t):
        out = np.zeros((t.shape[0], SIDE, LANES), np.float32)
        out[:, :size, :size] = t
        return out

    change = np.stack([change_matrix(S), change_matrix(S).T])
    return padded(table), padded(moved), padded(change)


def kernel(gz_count, ga, sol_ref, res_ref, dir_ref, gram_tab, moved_tab, change_tab,
           out_s, out_r, out_d,
           X, halo, stage, accs, red1, red2, coef, outbuf, fin,
           in_send, in_recv, own_sem, z_send, z_recv, r_send, r_recv,
           a_send, a_recv, b_send, b_recv, o_send, o_recv):
    group = 2 * ga
    groups = gz_count // 2
    planes, width, depth = sol_ref.shape
    tall = planes * group
    rows = width // group
    iz, ia = lax.axis_index("gz"), lax.axis_index("ga")
    g = iz // 2
    p = (iz % 2) * ga + ia

    def place(position):
        upper = position // ga
        return upper * (3 * ga - 1 - position) + (1 - upper) * position

    b = place(p)

    def device(which, position):
        return (which * 2 + position // ga, position % ga)

    def block_rows(block):
        return pl.ds(pl.multiple_of(block * rows, rows), rows)

    barrier = pltpu.get_barrier_semaphore()
    for j in range(1, group):
        pl.semaphore_signal(barrier, inc=1, device_id=device(g, (p + j) % group), device_id_type=MESH)
    for j in range(1, groups):
        pl.semaphore_signal(barrier, inc=1, device_id=device((g + j) % groups, p), device_id_type=MESH)
    pl.semaphore_wait(barrier, group - 1 + groups - 1)

    sources = (dir_ref, res_ref)

    def incoming(c, j):
        q = (p + j) % group
        return pltpu.make_async_remote_copy(
            src_ref=sources[c].at[:, block_rows(place(q)), :],
            dst_ref=X.at[c, 0, pl.ds(1 + planes * p, planes)],
            send_sem=in_send.at[c, j], recv_sem=in_recv.at[c, j],
            device_id=device(g, q), device_id_type=MESH)

    def own_in(c):
        return pltpu.make_async_copy(
            sources[c].at[:, block_rows(b), :],
            X.at[c, 0, pl.ds(1 + planes * p, planes)], own_sem.at[c])

    for c in range(2):
        for j in range(1, group):
            incoming(c, j).start()
        own_in(c).start()

    below, above = g > 0, g < groups - 1
    before, after = b > 0, b < group - 1

    @pl.when(g == 0)
    def _():
        for c in range(2):
            for k in range(S):
                X[c, k, 0] = jnp.zeros((rows, depth), jnp.float32)

    @pl.when(g == groups - 1)
    def _():
        for c in range(2):
            for k in range(S):
                X[c, k, tall + 1] = jnp.zeros((rows, depth), jnp.float32)

    @pl.when(b == 0)
    def _():
        for c in range(2):
            for k in range(S):
                halo[c, k, 0] = jnp.zeros((tall, depth), jnp.float32)

    @pl.when(b == group - 1)
    def _():
        for c in range(2):
            for k in range(S):
                halo[c, k, 1] = jnp.zeros((tall, depth), jnp.float32)

    def z_copy(c, k, up):
        return pltpu.make_async_remote_copy(
            src_ref=X.at[c, k, tall if up else 1],
            dst_ref=X.at[c, k, 0 if up else tall + 1],
            send_sem=z_send.at[c, k, up], recv_sem=z_recv.at[c, k, up],
            device_id=device(g + (1 if up else -1), p), device_id_type=MESH)

    def r_copy(c, k, up):
        return pltpu.make_async_remote_copy(
            src_ref=stage.at[c, k, up],
            dst_ref=halo.at[c, k, 1 - up],
            send_sem=r_send.at[c, k, up], recv_sem=r_recv.at[c, k, up],
            device_id=device(g, place(b + (1 if up else -1))), device_id_type=MESH)

    def send_z(c, k):
        @pl.when(below)
        def _():
            z_copy(c, k, 0).start()

        @pl.when(above)
        def _():
            z_copy(c, k, 1).start()

    def send_rows(c, k):
        @pl.when(before)
        def _():
            r_copy(c, k, 0).start()

        @pl.when(after)
        def _():
            r_copy(c, k, 1).start()

    def receive(c, k):
        @pl.when(before)
        def _():
            r_copy(c, k, 1).wait_recv()

        @pl.when(after)
        def _():
            r_copy(c, k, 0).wait_recv()

        @pl.when(below)
        def _():
            z_copy(c, k, 1).wait_recv()

        @pl.when(above)
        def _():
            z_copy(c, k, 0).wait_recv()

    row_ids = lax.broadcasted_iota(jnp.int32, (rows, depth), 0)
    col_ids = lax.broadcasted_iota(jnp.int32, (rows, depth), 1)
    first_row, last_row = row_ids == 0, row_ids == rows - 1
    first_col, last_col = col_ids == 0, col_ids == depth - 1

    def folded(x):
        total = x[0:8]
        for i in range(8, rows, 8):
            total = total + x[i:i + 8]
        out = total[:, 0:LANES]
        for i in range(LANES, depth, LANES):
            out = out + total[:, i:i + LANES]
        return out

    def chain_step(c, k):
        if c == 0:
            names = [(dd(k, 0), "new", "new"), (dd(k - 1, 1), "new", "cur")]
            if k == 1:
                names.append((dd(0, 0), "cur", "cur"))
            if k == S:
                names.append((dr(S - 1, 1), "new", "other"))
        else:
            names = [(rr(k, 0), "new", "new"), (rr(k - 1, 1), "new", "cur"),
                     (dr(k, 0), "new", "other"), (dr(k - 1, 1), "cur", "other")]
            if k == 1:
                names += [(rr(0, 0), "cur", "cur"), (dr(0, 0), "cur", "start")]

        def plane(z, sums):
            cur = X[c, k - 1, z + 1]
            total = X[c, k - 1, z] + X[c, k - 1, z + 2]
            low = halo[c, k - 1, 0, pl.ds(z, 1), :]
            high = halo[c, k - 1, 1, pl.ds(z, 1), :]
            total = total + jnp.where(first_row, low, pltpu.roll(cur, 1, 0))
            total = total + jnp.where(last_row, high, pltpu.roll(cur, rows - 1, 0))
            total = total + jnp.where(first_col, 0.0, pltpu.roll(cur, 1, 1))
            total = total + jnp.where(last_col, 0.0, pltpu.roll(cur, depth - 1, 1))
            if k == 1:
                new = total * first_scale
            else:
                new = total * next_scale - X[c, k - 2, z + 1]
            X[c, k, z + 1] = new
            if k < (S if c == 0 else S - 1):
                stage[c, k, 0, pl.ds(z, 1), :] = new[0:1]
                stage[c, k, 1, pl.ds(z, 1), :] = new[rows - 1:rows]
            have = {"new": new, "cur": cur}
            if any("other" in n for n in names):
                have["other"] = X[1, S - 1, z + 1] if c == 0 else X[0, k, z + 1]
            if any("start" in n for n in names):
                have["start"] = X[0, 0, z + 1]
            return tuple(s + folded(have[l] * have[r]) for s, (_, l, r) in zip(sums, names))

        more = k < (S if c == 0 else S - 1)
        sums = tuple(jnp.zeros((8, LANES), jnp.float32) for _ in names)
        sums = plane(0, sums)
        sums = plane(tall - 1, sums)
        if more:
            send_z(c, k)
        sums = lax.fori_loop(1, tall - 1, plane, sums, unroll=2)
        if more:
            send_rows(c, k)
        for s, (slot, _, _) in zip(sums, names):
            accs[slot] = s

    def arrive(c):
        own_in(c).wait()
        for j in range(1, group):
            incoming(c, j).wait_recv()
        send_z(c, 0)
        for z in range(tall):
            stage[c, 0, 0, z:z + 1, :] = X[c, 0, z + 1, 0:1, :]
            stage[c, 0, 1, z:z + 1, :] = X[c, 0, z + 1, rows - 1:rows, :]
        send_rows(c, 0)

    arrive(0)
    receive(0, 0)
    chain_step(0, 1)
    arrive(1)
    receive(1, 0)
    chain_step(1, 1)
    for k in range(2, S + 1):
        receive(0, k - 1)
        chain_step(0, k)
        if k < S:
            receive(1, k - 1)
            chain_step(1, k)

    lanes = lax.broadcasted_iota(jnp.int32, (8, LANES), 1)
    packed = jnp.zeros((8, LANES), jnp.float32)
    for t in range(COUNT // 8):
        part = jnp.sum(jnp.sum(accs[8 * t:8 * t + 8], axis=1), axis=1, keepdims=True)
        packed = packed + jnp.where(lanes == t, part, 0.0)
    red1[p] = packed

    def first_sum(j, mine):
        q = (p + j) % group
        slot = p if mine else q
        return pltpu.make_async_remote_copy(
            src_ref=red1.at[p], dst_ref=red1.at[slot],
            send_sem=a_send.at[j], recv_sem=a_recv.at[slot],
            device_id=device(g, q), device_id_type=MESH)

    def second_sum(j, mine):
        q = (g + j) % groups
        slot = g if mine else q
        return pltpu.make_async_remote_copy(
            src_ref=red2.at[g], dst_ref=red2.at[slot],
            send_sem=b_send.at[j], recv_sem=b_recv.at[slot],
            device_id=device(q, p), device_id_type=MESH)

    for j in range(1, group):
        first_sum(j, True).start()
    for j in range(1, group):
        first_sum(j, False).wait_recv()
    total = red1[0]
    for i in range(1, group):
        total = total + red1[i]
    red2[g] = total
    for j in range(1, groups):
        second_sum(j, True).start()
    for j in range(1, groups):
        second_sum(j, False).wait_recv()
    total = red2[0]
    for i in range(1, groups):
        total = total + red2[i]

    gram = jnp.zeros((SIDE, LANES), jnp.float32)
    moved = jnp.zeros((SIDE, LANES), jnp.float32)
    for e in range(COUNT):
        value = total[e % 8:e % 8 + 1, e // 8:e // 8 + 1]
        gram = gram + value * gram_tab[e]
        moved = moved + value * moved_tab[e]
    change, change_t = change_tab[0], change_tab[1]

    def full(x):
        return jnp.sum(jnp.sum(x, axis=0, keepdims=True), axis=1, keepdims=True)

    def unit(axis, at):
        ids = lax.broadcasted_iota(jnp.int32, (SIDE, LANES), axis)
        return jnp.where(ids == at, 1.0, 0.0).astype(jnp.float32)

    def inner(_, state):
        qc, qr, wc, wr, it, rho = state
        alpha = rho / full(qc * (moved * qr))
        mc = jnp.sum(change * qr, axis=1, keepdims=True)
        mr = jnp.sum(change_t * qc, axis=0, keepdims=True)
        it = it + alpha * qc
        wc = wc - alpha * mc
        wr = wr - alpha * mr
        rho_new = full(wc * (gram * wr))
        beta = rho_new / rho
        return wc + beta * qc, wr + beta * qr, wc, wr, it, rho_new

    wc, wr = unit(0, S + 1), unit(1, S + 1)
    state = (unit(0, 0), unit(1, 0), wc, wr, jnp.zeros((SIDE, LANES), jnp.float32),
             full(wc * (gram * wr)))
    qc, qr, wc, wr, it, rho = lax.fori_loop(0, S, inner, state)
    coef[0] = it
    coef[1] = wc
    coef[2] = qc

    def outgoing(j):
        q = (p + j) % group
        return pltpu.make_async_remote_copy(
            src_ref=outbuf.at[q],
            dst_ref=fin.at[:, :, block_rows(b), :],
            send_sem=o_send.at[j], recv_sem=o_recv.at[j],
            device_id=device(g, q), device_id_type=MESH)

    def outgoing_from(j):
        q = (p + group - j) % group
        return pltpu.make_async_remote_copy(
            src_ref=outbuf.at[q],
            dst_ref=fin.at[:, :, block_rows(place(q)), :],
            send_sem=o_send.at[j], recv_sem=o_recv.at[j],
            device_id=device(g, q), device_id_type=MESH)

    def combine(q):
        for i in range(planes):
            def strip(s, carry):
                at = pl.ds(pl.multiple_of(s * 16, 16), 16)
                sums = [None, None, None]
                for v in range(2 * S + 1):
                    c, k = (0, v) if v <= S else (1, v - S - 1)
                    x = X[c, k, planes * q + i + 1, at, :]
                    for o in range(3):
                        f = coef[o, v:v + 1, :]
                        f = jnp.concatenate([f] * (depth // LANES), axis=1)
                        term = f * x
                        sums[o] = term if sums[o] is None else sums[o] + term
                for o in range(3):
                    outbuf[q, o, i, at, :] = sums[o]
                return carry
            lax.fori_loop(0, rows // 16, strip, 0)

    for j in range(1, group):
        combine((p + j) % group)
        outgoing(j).start()
    combine(p)
    own_out = pltpu.make_async_copy(outbuf.at[p], fin.at[:, :, block_rows(b), :], own_sem.at[2])
    own_out.start()
    own_out.wait()
    for j in range(1, group):
        outgoing_from(j).wait_recv()

    out_s[...] = sol_ref[...] + fin[0]
    out_r[...] = fin[1]
    out_d[...] = fin[2]

    for c in range(2):
        for j in range(1, group):
            incoming(c, j).wait_send()
        for k in range(S if c == 0 else S - 1):
            @pl.when(below)
            def _():
                z_copy(c, k, 0).wait_send()

            @pl.when(above)
            def _():
                z_copy(c, k, 1).wait_send()

            @pl.when(before)
            def _():
                r_copy(c, k, 0).wait_send()

            @pl.when(after)
            def _():
                r_copy(c, k, 1).wait_send()
    for j in range(1, group):
        first_sum(j, True).wait_send()
        outgoing(j).wait_send()
    for j in range(1, groups):
        second_sum(j, True).wait_send()


def on_device(gz_count, ga, sol, res, direction):
    planes, width, depth = sol.shape
    group, groups = 2 * ga, gz_count // 2
    tall, rows = planes * group, width // group
    gram_tab, moved_tab, change_tab = (jnp.asarray(t) for t in gram_tables())
    vmem = pl.BlockSpec(memory_space=pltpu.VMEM)
    dma = pltpu.SemaphoreType.DMA
    shape = jax.ShapeDtypeStruct(sol.shape, jnp.float32)
    f32 = jnp.float32
    return pl.pallas_call(
        functools.partial(kernel, gz_count, ga),
        out_shape=(shape, shape, shape),
        in_specs=[vmem] * 6,
        out_specs=(vmem, vmem, vmem),
        scratch_shapes=[
            pltpu.VMEM((2, S + 1, tall + 2, rows, depth), f32),
            pltpu.VMEM((2, S, 2, tall, depth), f32),
            pltpu.VMEM((2, S, 2, tall, depth), f32),
            pltpu.VMEM((COUNT, 8, LANES), f32),
            pltpu.VMEM((group, 8, LANES), f32),
            pltpu.VMEM((groups, 8, LANES), f32),
            pltpu.VMEM((3, SIDE, LANES), f32),
            pltpu.VMEM((group, 3, planes, rows, depth), f32),
            pltpu.VMEM((3, planes, width, depth), f32),
            dma((2, group)), dma((2, group)), dma((3,)),
            dma((2, S, 2)), dma((2, S, 2)), dma((2, S, 2)), dma((2, S, 2)),
            dma((group,)), dma((group,)), dma((groups,)), dma((groups,)),
            dma((group,)), dma((group,)),
        ],
        compiler_params=pltpu.CompilerParams(collective_id=0, has_side_effects=True),
    )(sol, res, direction, gram_tab, moved_tab, change_tab)


def solution(mesh):
    spec = P(("gz", "ga"), None, None)
    return jax.shard_map(
        functools.partial(on_device, mesh.shape["gz"], mesh.shape["ga"]),
        mesh=mesh, in_specs=(spec, spec, spec), out_specs=(spec, spec, spec), check_vma=False,
    )
```

profile of v0, /device:TPU:1, one launch (start us, length us, event | category | flops | bytes accessed | tf_op | source)
XLA Modules:
  0.0 79.6 jit_solution(16319771970519692821)
XLA Ops:
  0.6 75.0 %shard_map.85 = (f32[2,256,256]{2,1,0:T(8,128)}, f32[2,256,256]{2,1,0:T(8,128)}, f32[2,256,256]{2,1,0:T(8,128)}) custom-call(f32[2,256,256]{2,1,0:T(8,128)} %sol_ref.1, f32[2,256,256]{2,1,0:T(8,128)} %res_ref.1, f32[2,256,256]{2,1,0:T(8,128)} %dir_ref.1, f32[48,24,128]{2,1,0:T(8,128)} %constant.6.clone.gram_tab, f32[48,24,128]{2,1,0:T(8,128)} %constant.7.clone.moved_tab, ...), custom_call_target="tpu_custom_call" | custom-call | tf_op jit(solution)/shard_map/pallas_call | solution.py:447
  75.6 0.0 copy-start.1
  75.6 1.9 %copy.12 = f32[2,256,256]{2,1,0:T(8,128)} copy(f32[2,256,256]{2,1,0:T(8,128)} %get-tuple-element.6) | data formatting | bytes 1048576
  77.5 0.0 copy-done.1
  77.5 0.0 copy-start
  77.5 0.8 copy.13
  78.3 0.4 copy-done
  78.8 0.8 copy.14
Async XLA Ops:
  75.6 1.9 %copy-start.1 = (f32[2,256,256]{2,1,0:T(8,128)S(1)}, f32[2,256,256]{2,1,0:T(8,128)}, u32[]{:S(2)}) copy-start(f32[2,256,256]{2,1,0:T(8,128)} %get-tuple-element.7) | copy-start | bytes 1572868
  77.5 1.2 %copy-start = (f32[2,256,256]{2,1,0:T(8,128)S(1)}, f32[2,256,256]{2,1,0:T(8,128)}, u32[]{:S(2)}) copy-start(f32[2,256,256]{2,1,0:T(8,128)} %get-tuple-element.8) | copy-start | bytes 1572868
where the time goes:
time: 79.8 us; the launch traced here: 79.6 us
  Pallas kernels  75 us (94%)
  local copies, waits for them, and re-layouts  3.95 us (5%)
    pallas_call x1, Pallas kernels, on_device(): pl.pallas_call(functools.partial(kernel, gz_count, ga), out_shape=(shape,...  75 us
    unnamed x7, local copies, waits for them, and re-layouts  3.95 us

commit v1 on v0

--- a/solution.py
+++ b/solution.py
@@ -72,14 +72,14 @@
     return padded(table), padded(moved), padded(change)
 
 
-def kernel(gz_count, ga, sol_ref, res_ref, dir_ref, gram_tab, moved_tab, change_tab,
-           out_s, out_r, out_d,
-           X, halo, stage, accs, red1, red2, coef, outbuf, fin,
+def kernel(gz_count, ga, res_ref, dir_ref, gram_hbm, moved_hbm, change_tab,
+           fin,
+           X, halo, stage, accs, red1, red2, coef, outbuf, held, gram_tab, moved_tab,
            in_send, in_recv, own_sem, z_send, z_recv, r_send, r_recv,
-           a_send, a_recv, b_send, b_recv, o_send, o_recv):
+           a_send, a_recv, b_send, b_recv, o_send, o_recv, load_sem):
     group = 2 * ga
     groups = gz_count // 2
-    planes, width, depth = sol_ref.shape
+    planes, width, depth = res_ref.shape
     tall = planes * group
     rows = width // group
     iz, ia = lax.axis_index("gz"), lax.axis_index("ga")
@@ -98,6 +98,11 @@
     def block_rows(block):
         return pl.ds(pl.multiple_of(block * rows, rows), rows)
 
+    loads = [pltpu.make_async_copy(source, target, load_sem.at[i]) for i, (source, target) in enumerate((
+        (dir_ref, held.at[0]), (res_ref, held.at[1]), (gram_hbm, gram_tab), (moved_hbm, moved_tab)))]
+    for load in loads:
+        load.start()
+
     barrier = pltpu.get_barrier_semaphore()
     for j in range(1, group):
         pl.semaphore_signal(barrier, inc=1, device_id=device(g, (p + j) % group), device_id_type=MESH)
@@ -105,22 +110,21 @@
         pl.semaphore_signal(barrier, inc=1, device_id=device((g + j) % groups, p), device_id_type=MESH)
     pl.semaphore_wait(barrier, group - 1 + groups - 1)
 
-    sources = (dir_ref, res_ref)
-
     def incoming(c, j):
         q = (p + j) % group
         return pltpu.make_async_remote_copy(
-            src_ref=sources[c].at[:, block_rows(place(q)), :],
+            src_ref=held.at[c, :, block_rows(place(q)), :],
             dst_ref=X.at[c, 0, pl.ds(1 + planes * p, planes)],
             send_sem=in_send.at[c, j], recv_sem=in_recv.at[c, j],
             device_id=device(g, q), device_id_type=MESH)
 
     def own_in(c):
         return pltpu.make_async_copy(
-            sources[c].at[:, block_rows(b), :],
+            held.at[c, :, block_rows(b), :],
             X.at[c, 0, pl.ds(1 + planes * p, planes)], own_sem.at[c])
 
     for c in range(2):
+        loads[c].wait()
         for j in range(1, group):
             incoming(c, j).start()
         own_in(c).start()
@@ -220,11 +224,11 @@
             names = [(dd(k, 0), "new", "new"), (dd(k - 1, 1), "new", "cur")]
             if k == 1:
                 names.append((dd(0, 0), "cur", "cur"))
-            if k == S:
-                names.append((dr(S - 1, 1), "new", "other"))
         else:
             names = [(rr(k, 0), "new", "new"), (rr(k - 1, 1), "new", "cur"),
                      (dr(k, 0), "new", "other"), (dr(k - 1, 1), "cur", "other")]
+            if k == S - 1:
+                names.append((dr(k, 1), "new", "ahead"))
             if k == 1:
                 names += [(rr(0, 0), "cur", "cur"), (dr(0, 0), "cur", "start")]
 
@@ -247,7 +251,9 @@
                 stage[c, k, 1, pl.ds(z, 1), :] = new[rows - 1:rows]
             have = {"new": new, "cur": cur}
             if any("other" in n for n in names):
-                have["other"] = X[1, S - 1, z + 1] if c == 0 else X[0, k, z + 1]
+                have["other"] = X[0, k, z + 1]
+            if any("ahead" in n for n in names):
+                have["ahead"] = X[0, k + 1, z + 1]
             if any("start" in n for n in names):
                 have["start"] = X[0, 0, z + 1]
             return tuple(s + folded(have[l] * have[r]) for s, (_, l, r) in zip(sums, names))
@@ -258,7 +264,7 @@
         sums = plane(tall - 1, sums)
         if more:
             send_z(c, k)
-        sums = lax.fori_loop(1, tall - 1, plane, sums, unroll=2)
+        sums = lax.fori_loop(1, tall - 1, plane, sums, unroll=7)
         if more:
             send_rows(c, k)
         for s, (slot, _, _) in zip(sums, names):
@@ -277,15 +283,15 @@
     arrive(0)
     receive(0, 0)
     chain_step(0, 1)
+    receive(0, 1)
+    chain_step(0, 2)
     arrive(1)
-    receive(1, 0)
-    chain_step(1, 1)
-    for k in range(2, S + 1):
-        receive(0, k - 1)
-        chain_step(0, k)
-        if k < S:
-            receive(1, k - 1)
-            chain_step(1, k)
+    for k in range(1, S):
+        receive(1, k - 1)
+        chain_step(1, k)
+        if k + 2 <= S:
+            receive(0, k + 1)
+            chain_step(0, k + 2)
 
     lanes = lax.broadcasted_iota(jnp.int32, (8, LANES), 1)
     packed = jnp.zeros((8, LANES), jnp.float32)
@@ -326,6 +332,8 @@
     for i in range(1, groups):
         total = total + red2[i]
 
+    loads[2].wait()
+    loads[3].wait()
     gram = jnp.zeros((SIDE, LANES), jnp.float32)
     moved = jnp.zeros((SIDE, LANES), jnp.float32)
     for e in range(COUNT):
@@ -405,10 +413,6 @@
     for j in range(1, group):
         outgoing_from(j).wait_recv()
 
-    out_s[...] = sol_ref[...] + fin[0]
-    out_r[...] = fin[1]
-    out_d[...] = fin[2]
-
     for c in range(2):
         for j in range(1, group):
             incoming(c, j).wait_send()
@@ -442,13 +446,14 @@
     gram_tab, moved_tab, change_tab = (jnp.asarray(t) for t in gram_tables())
     vmem = pl.BlockSpec(memory_space=pltpu.VMEM)
     dma = pltpu.SemaphoreType.DMA
-    shape = jax.ShapeDtypeStruct(sol.shape, jnp.float32)
+    shape = jax.ShapeDtypeStruct((3,) + sol.shape, jnp.float32)
+    anywhere = pl.BlockSpec(memory_space=pl.ANY)
     f32 = jnp.float32
-    return pl.pallas_call(
+    combined = pl.pallas_call(
         functools.partial(kernel, gz_count, ga),
-        out_shape=(shape, shape, shape),
-        in_specs=[vmem] * 6,
-        out_specs=(vmem, vmem, vmem),
+        out_shape=shape,
+        in_specs=[anywhere] * 4 + [vmem],
+        out_specs=vmem,
         scratch_shapes=[
             pltpu.VMEM((2, S + 1, tall + 2, rows, depth), f32),
             pltpu.VMEM((2, S, 2, tall, depth), f32),
@@ -458,14 +463,17 @@
             pltpu.VMEM((groups, 8, LANES), f32),
             pltpu.VMEM((3, SIDE, LANES), f32),
             pltpu.VMEM((group, 3, planes, rows, depth), f32),
-            pltpu.VMEM((3, planes, width, depth), f32),
+            pltpu.VMEM((2, planes, width, depth), f32),
+            pltpu.VMEM((COUNT, SIDE, LANES), f32),
+            pltpu.VMEM((COUNT, SIDE, LANES), f32),
             dma((2, group)), dma((2, group)), dma((3,)),
             dma((2, S, 2)), dma((2, S, 2)), dma((2, S, 2)), dma((2, S, 2)),
             dma((group,)), dma((group,)), dma((groups,)), dma((groups,)),
-            dma((group,)), dma((group,)),
+            dma((group,)), dma((group,)), dma((4,)),
         ],
         compiler_params=pltpu.CompilerParams(collective_id=0, has_side_effects=True),
-    )(sol, res, direction, gram_tab, moved_tab, change_tab)
+    )(res, direction, gram_tab, moved_tab, change_tab)
+    return sol + combined[0], combined[1], combined[2]
 
 
 def solution(mesh):

time: 79.8 us -> 78.9 us (0.989)
  other arithmetic: 0 us -> 1.9 us
  local copies, waits for them, and re-layouts: 3.95 us -> 2.32 us
  Pallas kernels: 75 us -> 73.7 us
    unnamed x7 -> x2, local copies, waits for them, and re-layouts: 3.95 us -> 0.01 us
    squeeze x0 -> x1, local copies, waits for them, and re-layouts: none -> 2.31 us  [on_device(): return (sol + combined[0], combined[1], combined[2])]
    add x0 -> x1, other arithmetic: none -> 1.9 us  [on_device(): return (sol + combined[0], combined[1], combined[2])]
    pallas_call x1, Pallas kernels: 75 us -> 73.7 us  [on_device(): pl.pallas_call(functools.partial(kernel, gz_count, ga), out_shape=shape,...]
where the time goes in v1:
time: 78.9 us; the launch traced here: 78.6 us
  Pallas kernels  73.7 us (93%)
  local copies, waits for them, and re-layouts  2.32 us (3%)
  other arithmetic  1.9 us (2%)
    pallas_call x1, Pallas kernels, on_device(): pl.pallas_call(functools.partial(kernel, gz_count, ga), out_shape=shape,...  73.7 us
    squeeze x1, local copies, waits for them, and re-layouts, on_device(): return (sol + combined[0], combined[1], combined[2])  2.31 us
    add x1, other arithmetic, on_device(): return (sol + combined[0], combined[1], combined[2])  1.9 us

profile of v1, /device:TPU:1, one launch (start us, length us, event | category | flops | bytes accessed | tf_op | source)
XLA Modules:
  0.0 78.6 jit_solution(3192132774643231911)
XLA Ops:
  0.6 73.7 %shard_map.85 = f32[3,2,256,256]{3,2,1,0:T(8,128)} custom-call(f32[2,256,256]{2,1,0:T(8,128)} %res_ref.1, f32[2,256,256]{2,1,0:T(8,128)} %dir_ref.1, f32[48,24,128]{2,1,0:T(8,128)} %constant.6.clone.gram_hbm, f32[48,24,128]{2,1,0:T(8,128)} %constant.7.clone.moved_hbm, f32[2,24,128]{2,1,0:T(8,128)} %constant.8.clone.change_tab), custom_call_target="tpu_custom_call" | custom-call | tf_op jit(solution)/shard_map/pallas_call | solution.py:452
  74.4 0.0 copy-start
  74.4 2.3 %slice_bitcast_fusion = (f32[2,256,256]{2,1,0:T(8,128)}, f32[2,256,256]{2,1,0:T(8,128)}) fusion(f32[3,2,256,256]{3,2,1,0:T(8,128)} %shard_map.85), kind=kLoop, calls=%fused_computation.1 | loop fusion | bytes 2097152 | tf_op jit(solution)/shard_map/squeeze | solution.py:476
  76.7 0.0 copy-done
  76.7 1.9 %bitcast_add_fusion = f32[2,256,256]{2,1,0:T(8,128)} fusion(f32[2,256,256]{2,1,0:T(8,128)S(1)} %copy-done, f32[3,2,256,256]{3,2,1,0:T(8,128)} %shard_map.85), kind=kLoop, calls=%fused_computation | loop fusion | flops 131072 | bytes 1572864 | tf_op jit(solution)/shard_map/add | solution.py:476
Async XLA Ops:
  74.4 2.3 %copy-start = (f32[2,256,256]{2,1,0:T(8,128)S(1)}, f32[2,256,256]{2,1,0:T(8,128)}, u32[]{:S(2)}) copy-start(f32[2,256,256]{2,1,0:T(8,128)} %param.6) | copy-start | bytes 1572868
